TPU v7x, 32 devices: a whole 2x2x4 slice. The times are simulated.
32 devices in a mesh: gx: 2 (over x), gy: 4 (over z), gz: 4 (over y, core).
Axes of the slice: x: 2, y: 2, z: 4, core: 2. Of those that a mesh axis runs over, the one named last changes fastest.
Arguments:
- state_old: float32 [5, 32, 128, 512], P(None, 'gx', 'gy', 'gz'), as said below
- state_section: float32 [5, 32, 128, 512], P(None, 'gx', 'gy', 'gz'), as said below
- panel_record: bfloat16 [131072, 512], P(('gx', 'gy', 'gz')), may hold values from -6 to 6
- panel_cell: int32 [1024, 128], P(('gx', 'gy', 'gz')), may hold values from 0 to 65535
- panel_angles: float32 [2, 131072], P(None, ('gx', 'gy', 'gz')), may hold values from -3.140625 to 3.140625
- owned_blocks: int32 [32], P(('gx', 'gy', 'gz')), may hold values from 1 to 32, 256 in all
- listener_angles: float32 [2, 1024], replicated, may hold values from -3.140625 to 3.140625
- listener_range: float32 [1024], replicated, may hold values from 1.2 to 2.5
Outputs:
- state_next: float32 [5, 32, 128, 512], P(None, 'gx', 'gy', 'gz')
- observer_spectra: float32 [2, 1024, 128], P(None, 'gz')
Inputs may be any that keep to these rules, and one draw needn't show every extreme that they name: `state_old`: density between 0.5 and 2, velocity components of magnitude 0.3 at most, stiffened-gas pressure between 0.3 and 2. `state_section`: density between 0.5 and 2, velocity components of magnitude 0.3 at most, stiffened-gas pressure between 0.3 and 2. A device's live blocks fill its first owned_blocks slots; some device owns 32 blocks, and they total 8 times the number of devices.
All inputs are finite; a program needn't handle non-finite values.
Results may differ from a plain program's by a relative error of at most 0.0003.
The roundings to bfloat16 on the way count: a program that leaves them out, or rounds other values in their place, can miss the bound.
Values may be sent and summed in bfloat16 or wider, within the bound.
No kernel may reach another device: no remote copies, remote signals or barrier semaphores. Data moves between devices by JAX's collectives and lax.ppermute only.
A program may use at most 64 MiB of HBM per device.

v0:
```python
import math
import jax
import jax.numpy as jnp
from jax import lax
from jax.sharding import PartitionSpec as P

FREQS = 128
GROUP = 4
GAMMA_GAS = 4.4
PRESSURE_INF = 1.0
WENO_EPS = 1e-06
WAVE_STEP = 0.25
COURANT = 0.08


def with_halo(shard, sides, width):
    for axis, dim in sides:
        size, length = (lax.axis_size(axis), shard.shape[dim])
        up = [(i, (i + 1) % size) for i in range(size)]
        down = [(j, i) for i, j in up]
        last = lax.slice_in_dim(shard, length - width, length, axis=dim)
        initial = lax.slice_in_dim(shard, 0, width, axis=dim)
        before = lax.ppermute(last, axis, up)
        after = lax.ppermute(initial, axis, down)
        shard = jnp.concatenate([before, shard, after], axis=dim)
    return shard


def weno_face(far_left, near_left, middle, near_right, far_right):
    cand_a = (2.0 * far_left - 7.0 * near_left + 11.0 * middle) / 6.0
    cand_b = (-near_left + 5.0 * middle + 2.0 * near_right) / 6.0
    cand_c = (2.0 * middle + 5.0 * near_right - far_right) / 6.0
    rough_a = (
        13.0 / 12.0 * (far_left - 2.0 * near_left + middle) ** 2
        + 0.25 * (far_left - 4.0 * near_left + 3.0 * middle) ** 2
    )
    rough_b = (
        13.0 / 12.0 * (near_left - 2.0 * middle + near_right) ** 2
        + 0.25 * (near_left - near_right) ** 2
    )
    rough_c = (
        13.0 / 12.0 * (middle - 2.0 * near_right + far_right) ** 2
        + 0.25 * (3.0 * middle - 4.0 * near_right + far_right) ** 2
    )
    weight_a = 0.1 / (WENO_EPS + rough_a) ** 2
    weight_b = 0.6 / (WENO_EPS + rough_b) ** 2
    weight_c = 0.3 / (WENO_EPS + rough_c) ** 2
    return (weight_a * cand_a + weight_b * cand_b + weight_c * cand_c) / (
        weight_a + weight_b + weight_c
    )


def euler_flux(state_slab, axis_d):
    density = state_slab[0]
    momenta = state_slab[1:4]
    energy = state_slab[4]
    velocity = momenta / density[None]
    kinetic = 0.5 * jnp.sum(momenta * velocity, axis=0)
    pressure = (GAMMA_GAS - 1.0) * (energy - kinetic) - GAMMA_GAS * PRESSURE_INF
    normal_speed = velocity[axis_d]
    sound_speed = jnp.sqrt(GAMMA_GAS * (pressure + PRESSURE_INF) / density)
    rows_out = [momenta[axis_d]]
    for component in range(3):
        carried = momenta[component] * normal_speed
        if component == axis_d:
            carried = carried + pressure
        rows_out.append(carried)
    rows_out.append((energy + pressure) * normal_speed)
    return (jnp.stack(rows_out), jnp.abs(normal_speed) + sound_speed)


def face_difference(padded, axis_d, count_d):
    array_axis = axis_d + 1
    picker = [slice(None), slice(3, -3), slice(3, -3), slice(3, -3)]
    picker[array_axis] = slice(None)
    state_slab = padded[tuple(picker)]
    fluxes, speeds = euler_flux(state_slab, axis_d)
    cell_count = state_slab.shape[array_axis] - 6

    def shifted(values, offset, along):
        return lax.slice_in_dim(values, offset, offset + cell_count + 1, axis=along)

    wave_speed = shifted(speeds, 0, axis_d)
    for offset in range(1, 6):
        wave_speed = jnp.maximum(wave_speed, shifted(speeds, offset, axis_d))
    split_up = [
        0.5
        * (
            shifted(fluxes, offset, array_axis)
            + wave_speed[None] * shifted(state_slab, offset, array_axis)
        )
        for offset in range(6)
    ]
    split_down = [
        0.5
        * (
            shifted(fluxes, offset, array_axis)
            - wave_speed[None] * shifted(state_slab, offset, array_axis)
        )
        for offset in range(6)
    ]
    face_flux = weno_face(
        split_up[0], split_up[1], split_up[2], split_up[3], split_up[4]
    ) + weno_face(split_down[5], split_down[4], split_down[3], split_down[2], split_down[1])
    after = lax.slice_in_dim(face_flux, 1, cell_count + 1, axis=array_axis)
    before = lax.slice_in_dim(face_flux, 0, cell_count, axis=array_axis)
    return (after - before) * float(count_d)


def section_update(padded, old_block, counts, step_size):
    change = (
        face_difference(padded, 0, counts[0])
        + face_difference(padded, 1, counts[1])
        + face_difference(padded, 2, counts[2])
    )
    return 0.75 * old_block + 0.25 * (padded[:, 3:-3, 3:-3, 3:-3] - step_size * change)


def directions(angles):
    polar_angle = 0.5 * angles[0]
    azimuth = angles[1]
    return jnp.stack(
        [
            jnp.cos(polar_angle) * jnp.cos(azimuth),
            jnp.cos(polar_angle) * jnp.sin(azimuth),
            jnp.sin(polar_angle),
        ]
    )


def panel_places(cell_rows, block_x, block_y, block_z, cells_x, cells_y, cells_z, counts):
    along_x = cell_rows // (cells_y * cells_z)
    along_y = cell_rows // cells_z % cells_y
    along_z = cell_rows % cells_z
    place_x = ((block_x * cells_x + along_x).astype(jnp.float32) + 0.5) / counts[0]
    place_y = ((block_y * cells_y + along_y).astype(jnp.float32) + 0.5) / counts[1]
    place_z = ((block_z * cells_z + along_z).astype(jnp.float32) + 0.5) / counts[2]
    return jnp.stack([place_x, place_y, place_z], axis=1)


def dft_table(sample_count, freq_count):
    times = jnp.arange(sample_count, dtype=jnp.int32)[:, None]
    orders = jnp.arange(1, freq_count + 1, dtype=jnp.int32)[None, :]
    phases = 2.0 * math.pi / sample_count * (times * orders % sample_count).astype(jnp.float32)
    scaling = 1.0 / math.sqrt(sample_count)
    return (jnp.concatenate([jnp.cos(phases), -jnp.sin(phases)], axis=1) * scaling).astype(
        jnp.bfloat16
    )


def observer_group(sources, geometry, live_flags, dft_rows, listeners, wave_numbers):
    places = geometry[:, 0:3]
    normals = geometry[:, 3:6]
    spectra = jnp.einsum(
        "gpt,tk->gpk", sources, dft_rows, preferred_element_type=jnp.float32
    ).astype(jnp.bfloat16)
    offsets = listeners[None, :, :, None] - places[:, :, None, :]
    dist_sq = jnp.sum(offsets * offsets, axis=1)
    facing = jnp.sum(normals[:, :, None, :] * offsets, axis=1)
    weights = (facing / (4.0 * math.pi * dist_sq)).astype(jnp.bfloat16)
    product = jnp.einsum("gop,gpk->gok", weights, spectra, preferred_element_type=jnp.float32)
    centres = jnp.mean(places, axis=2)
    separation = listeners[None, :, :] - centres[:, :, None]
    centre_reach = jnp.sqrt(jnp.sum(separation * separation, axis=1))
    phase_now = centre_reach[:, :, None] * wave_numbers[None, None, :]
    cosine = jnp.cos(phase_now)
    sine_part = jnp.sin(phase_now)
    freq_count = wave_numbers.shape[0]
    real_part = product[:, :, :freq_count] * cosine + product[:, :, freq_count:] * sine_part
    imag_part = product[:, :, freq_count:] * cosine - product[:, :, :freq_count] * sine_part
    masks = live_flags[:, None, None]
    return jnp.stack([jnp.sum(masks * real_part, axis=0), jnp.sum(masks * imag_part, axis=0)])


def local(
    state_old,
    state_section,
    panel_record,
    panel_cell,
    panel_angles,
    owned_blocks,
    listener_angles,
    listener_range,
):
    cells_x = state_section.shape[1]
    cells_y = state_section.shape[2]
    cells_z = state_section.shape[3]
    counts = (
        cells_x * lax.axis_size("gx"),
        cells_y * lax.axis_size("gy"),
        cells_z * lax.axis_size("gz"),
    )
    step_size = COURANT / max(counts)
    padded = with_halo(state_section, (("gx", 1), ("gy", 2), ("gz", 3)), 3)
    updated = section_update(padded, state_old, counts, step_size)
    slot_count = panel_cell.shape[0]
    block_rows = panel_cell.shape[1]
    samples = panel_record.shape[1]
    density = updated[0].reshape(cells_x * cells_y * cells_z)
    sampled = density[panel_cell]
    sources = (
        panel_record.reshape(slot_count, block_rows, samples).astype(jnp.float32)
        * sampled[:, :, None]
    ).astype(jnp.bfloat16)
    places = panel_places(
        panel_cell,
        lax.axis_index("gx"),
        lax.axis_index("gy"),
        lax.axis_index("gz"),
        cells_x,
        cells_y,
        cells_z,
        counts,
    )
    normals = jnp.transpose(directions(panel_angles.reshape(2, slot_count, block_rows)), (1, 0, 2))
    geometry = jnp.concatenate([places, normals], axis=1)
    live_count = owned_blocks[0]
    live_flags = (jnp.arange(slot_count, dtype=jnp.int32) < live_count).astype(jnp.float32)
    dft_rows = dft_table(samples, FREQS)
    listeners = 0.5 + listener_range[None, :] * directions(listener_angles)
    wave_numbers = WAVE_STEP * jnp.arange(1, FREQS + 1, dtype=jnp.int32).astype(jnp.float32)

    def add_group(group_turn, running):
        first_row = group_turn * GROUP
        group_sources = lax.dynamic_slice_in_dim(sources, first_row, GROUP, 0)
        group_geometry = lax.dynamic_slice_in_dim(geometry, first_row, GROUP, 0)
        group_flags = lax.dynamic_slice_in_dim(live_flags, first_row, GROUP, 0)
        return running + observer_group(
            group_sources, group_geometry, group_flags, dft_rows, listeners, wave_numbers
        )

    group_total = (live_count + GROUP - 1) // GROUP
    running = lax.fori_loop(
        0, group_total, add_group, jnp.zeros((2, listeners.shape[1], FREQS), jnp.float32)
    )
    gz_share = lax.psum_scatter(running, "gz", scatter_dimension=1, tiled=True)
    spectra_out = lax.psum(gz_share, ("gx", "gy"))
    return (updated, spectra_out)


def solution(mesh):
    return jax.shard_map(
        local,
        mesh=mesh,
        in_specs=(
            P(None, "gx", "gy", "gz"),
            P(None, "gx", "gy", "gz"),
            P(("gx", "gy", "gz"), None),
            P(("gx", "gy", "gz"), None),
            P(None, ("gx", "gy", "gz")),
            P(("gx", "gy", "gz")),
            P(),
            P(),
        ),
        out_specs=(P(None, "gx", "gy", "gz"), P(None, "gz", None)),
        check_vma=False,
    )
```

profile of v0, /device:TPU:0, one launch (start us, length us, event | category | flops | bytes accessed | tf_op | source)
XLA Modules:
  0.0 392.4 jit_solution(911386908631650255)
XLA Ops:
  7.2 1.9 fusion.121
  9.1 3.0 collective-permute-start
  12.8 1.8 multiply_bitcast_fusion.1
  14.6 1.0 cosine_multiply_fusion
  15.6 1.1 fusion.95
  20.3 3.0 collective-permute-done.1
  24.4 1.9 collective-permute-start.2
  26.3 2.1 collective-permute-start.3
  28.4 7.8 %divide_add_fusion.2 = f32[5,17,32,128]{3,2,1,0:T(8,128)} fusion(f32[5,19,32,128]{3,2,1,0:T(8,128)S(1)} %get-tuple-element.123, f32[5,22,32,128]{3,2,1,0:T(8,128)S(1)} %multiply_dynamic-update-slice_fusion.1, f32[5,19,32,128]{3,2,1,0:T(8,128)S(1)} %get-tuple-element.116, f32[17,32,128]{2,1,0:T(8,128)S(1)} %slice_maximum_fusion.10), kind=kLoop, calls=%fused_computation.92 | loop fusion | flops 51179520 | bytes 18382848 | tf_op jit(solution)/shard_map/add | solution.py:102
  36.2 1.0 collective-permute-done.3
  38.0 2.7 fusion.119
  42.2 3.3 copy.41
  45.5 3.3 copy.42
  48.7 1.7 collective-permute-start.5
  50.5 11.8 %divide_add_fusion.1 = f32[5,16,33,128]{3,2,1,0:T(8,128)} fusion(f32[5,22,3,128]{3,2,1,0:T(4,128)} %copy-done.5, f32[5,22,32,128]{3,2,1,0:T(8,128)S(1)} %get-tuple-element.124, f32[5,16,38,128]{3,2,1,0:T(8,128)S(1)} %multiply_dynamic-update-slice_fusion.2, f32[5,22,3,128]{3,2,1,0:T(4,128)} %copy-done.3, f32[16,33,128]{2,1,0:T(8,128)} %slice_maximum_fusion.5), kind=kLoop, calls=%fused_computation.75 | loop fusion | flops 51701760 | bytes 11872256 | tf_op jit(solution)/shard_map/add | solution.py:102
  62.3 3.2 copy.43
  65.5 3.2 copy.44
  68.7 4.9 %pad_maximum_fusion = f32[5,22,38,134]{3,2,1,0:T(8,128)S(1)} fusion(f32[5,22,38,3]{3,2,1,0:T(8,128)} %copy.44, f32[5,22,3,128]{3,2,1,0:T(4,128)S(1)} %copy-done.6, f32[5,22,32,128]{3,2,1,0:T(8,128)S(1)} %get-tuple-element.124, f32[5,22,3,128]{3,2,1,0:T(4,128)S(1)} %copy-done.4, f32[5,22,38,3]{3,2,1,0:T(8,128)} %copy.43), kind=kLoop, calls=%fused_computation.34 | loop fusion | flops 2240480 | bytes 4480960 | tf_op jit(solution)/shard_map/concatenate | solution.py:25
  76.8 2.8 maximum_maximum_fusion
  79.6 15.3 %divide_add_fusion = f32[5,16,32,129]{3,2,1,0:T(8,128)S(1)} fusion(f32[5,22,38,131]{3,2,1,0:T(8,128)S(1)} %get-tuple-element.109, f32[5,16,32,134]{3,2,1,0:T(8,128)S(1)} %multiply_dynamic-update-slice_fusion, f32[5,22,38,131]{3,2,1,0:T(8,128)S(1)} %get-tuple-element.108, f32[16,32,129]{2,1,0:T(8,128)S(1)} %slice_maximum_fusion), kind=kLoop, calls=%fused_computation.49 | loop fusion | flops 48545280 | bytes 17436672 | tf_op jit(solution)/shard_map/add | solution.py:102
  95.8 23.0 %gather_fusion = f32[4096]{0:T(1024)S(1)} fusion(f32[65536]{0:T(1024)S(1)} %bitcast.126, s32[4096]{0:T(1024)S(1)} %fusion.111), kind=kCustom, calls=%fused_computation | custom fusion | bytes 49152 | tf_op jit(solution)/shard_map/gather | solution.py:200
  118.9 4.1 %fusion.23 = bf16[32,128,512]{2,1,0:T(8,128)(2,1)} fusion(bf16[32,128,512]{2,1,0:T(8,128)(2,1)} %bitcast.129, f32[32,128]{1,0:T(8,128)S(1)} %bitcast.133), kind=kLoop, calls=%fused_computation.33 | loop fusion | flops 6291456 | bytes 8404992 | tf_op jit(solution)/shard_map/convert_element_type | solution.py:204
  123.1 40.5 %while.11 = (s32[]{:T(128)}, f32[2,1024,128]{2,1,0:T(8,128)S(1)}, s32[]{:T(128)}, f32[32]{0:T(128)S(1)}, f32[32,6,128]{2,1,0:T(8,128)}, /*index=5*/f32[3,1024]{1...) while((s32[]{:T(128)}, f32[2,1024,128]{2,1,0:T(8,128)S(1)}, ...), condition=%wide.region_10.11_spmd.clone, body=%wide.region_3.10_spmd.clone.sunk | while | flops 417236864 | bytes 21886488 | solution.py:233
  124.2 2.9 fusion.131
  127.1 4.8 %fusion.132 = f32[4,1024,256]{2,1,0:T(8,128)} fusion(f32[4,1024,128]{2,1,0:T(8,128)} %get-tuple-element.195, f32[4,1024,128]{2,1,0:T(8,128)S(1)} %get-tuple-element.196, bf16[32,128,512]{2,1,0:T(8,128)(2,1)} %get-tuple-element.232, s32[]{:T(128)S(6)} %select_n.94, bf16[512,256]{1,0:T(8,128)(2,1)S(1)} %get-tuple-element.233), kind=kOutput, calls=%fused_computation.20.clone.1 | convolution fusion | flops 404357120 | bytes 9175044 | tf_op jit(solution)/shard_map/while/body/gop,gpk->gok/dot_general | solution.py:161
  132.2 11.0 %fusion.133 = (f32[1024,128]{1,0:T(8,128)S(1)}, f32[1024,128]{1,0:T(8,128)S(1)}) fusion(f32[4,1024,256]{2,1,0:T(8,128)} %fusion.132, f32[128]{0:T(128)S(1)} %convert_multiply_fusion.3, f32[4,1024]{1,0:T(4,128)S(1)} %sqrt.30, f32[4]{0:T(128)S(1)} %dynamic_slice.18), kind=kLoop, calls=%fused_computation.14.clone.1 | loop fusion | flops 5505024 | bytes 5259792 | tf_op jit(solution)/shard_map/while/body/reduce_sum | solution.py:172
  144.3 2.9 fusion.131
  147.3 4.8 %fusion.132 = f32[4,1024,256]{2,1,0:T(8,128)} fusion(f32[4,1024,128]{2,1,0:T(8,128)} %get-tuple-element.195, f32[4,1024,128]{2,1,0:T(8,128)S(1)} %get-tuple-element.196, bf16[32,128,512]{2,1,0:T(8,128)(2,1)} %get-tuple-element.232, s32[]{:T(128)S(6)} %select_n.94, bf16[512,256]{1,0:T(8,128)(2,1)S(1)} %get-tuple-element.233), kind=kOutput, calls=%fused_computation.20.clone.1 | convolution fusion | flops 404357120 | bytes 9175044 | tf_op jit(solution)/shard_map/while/body/gop,gpk->gok/dot_general | solution.py:161
  152.4 11.0 %fusion.133 = (f32[1024,128]{1,0:T(8,128)S(1)}, f32[1024,128]{1,0:T(8,128)S(1)}) fusion(f32[4,1024,256]{2,1,0:T(8,128)} %fusion.132, f32[128]{0:T(128)S(1)} %convert_multiply_fusion.3, f32[4,1024]{1,0:T(4,128)S(1)} %sqrt.30, f32[4]{0:T(128)S(1)} %dynamic_slice.18), kind=kLoop, calls=%fused_computation.14.clone.1 | loop fusion | flops 5505024 | bytes 5259792 | tf_op jit(solution)/shard_map/while/body/reduce_sum | solution.py:172
  164.7 144.8 %reduce-scatter.2.cloned.1.call-done = f32[2,256,128]{2,1,0:T(8,128)} async-done(((f32[2,1024,128]{2,1,0:T(8,128)}), f32[2,256,128]{2,1,0:T(8,128)}) %reduce-scatter.2.cloned.1.call-update) | async-done | bytes 262160 | tf_op jit(solution)/shard_map/reduce_scatter | solution.py:236
  309.5 74.4 %all-reduce.2.cloned.1.call-done = f32[2,256,128]{2,1,0:T(8,128)} async-done(((f32[2,256,128]{2,1,0:T(8,128)}), f32[2,256,128]{2,1,0:T(8,128)}) %all-reduce.2.cloned.1.call-update) | async-done | bytes 262160 | tf_op jit(solution)/shard_map/psum | solution.py:237
  383.9 1.7 copy.75
  (98 shorter events, 14.7 us)
Async XLA Ops:
  7.2 12.8 %copy-start.10 = (f32[5,16,32,128]{3,2,1,0:T(8,128)S(1)}, f32[5,16,32,128]{3,2,1,0:T(8,128)}, u32[]{:S(2)}) copy-start(f32[5,16,32,128]{3,2,1,0:T(8,128)} %param.11) | copy-start | bytes 3932164
  7.2 10.3 %copy-start.14 = (s32[32,128]{1,0:T(8,128)S(1)}, s32[32,128]{1,0:T(8,128)}, u32[]{:S(2)}) copy-start(s32[32,128]{1,0:T(8,128)} %param.13) | copy-start | bytes 49156
  7.2 11.1 %copy-start.15 = (f32[1024]{0:T(1024)S(1)}, f32[1024]{0:T(1024)}, u32[]{:S(2)}) copy-start(f32[1024]{0:T(1024)} %param.17) | copy-start | bytes 12292
  7.2 302.3 %reduce-scatter.2.cloned.1.call-start = ((), (), s32[]{:S(2)}) async-start(), calls=%async_computation.1 | async-start | bytes 1310720 | tf_op jit(solution)/shard_map/reduce_scatter | solution.py:236
  9.1 9.9 %collective-permute-start = (f32[5,3,32,128]{3,2,1,0:T(8,128)S(1)}, f32[5,3,32,128]{3,2,1,0:T(8,128)}, u32[]{:S(2)}, u32[]{:S(2)}) collective-permute-start(f32[5,3,32,128]{3,2,1,0:T(8,128)S(1)} %get-tuple-element.120), channel_id=1, source_target_pairs={{0,16},{16,0},{1,17},{17,1},{2,18},{18,2},{3,19},{19,3},{4,20},{20... | collective-permute-start | bytes 737288 | tf_op jit(solution)/shard_map/ppermute | solution.py:23
  12.1 11.2 %collective-permute-start.1 = (f32[5,3,32,128]{3,2,1,0:T(8,128)}, f32[5,3,32,128]{3,2,1,0:T(8,128)S(1)}, u32[]{:S(2)}, u32[]{:S(2)}) collective-permute-start(f32[5,3,32,128]{3,2,1,0:T(8,128)} %get-tuple-element.119), channel_id=1, source_target_pairs={{16,0},{0,16},{17,1},{1,17},{18,2},{2,18},{19,3},{3,19},{20,4},{4,... | collective-permute-start | bytes 737288 | tf_op jit(solution)/shard_map/ppermute | solution.py:24
  24.4 11.8 %collective-permute-start.2 = (f32[5,22,3,128]{3,2,1,0:T(4,128)S(1)}, f32[5,22,3,128]{3,2,1,0:T(4,128)S(1)}, u32[]{:S(2)}, u32[]{:S(2)}) collective-permute-start(f32[5,22,3,128]{3,2,1,0:T(4,128)S(1)} %get-tuple-element.114), channel_id=1, source_target_pairs={{0,4},{4,8},{8,12},{12,0},{1,5},{5,9},{9,13},{13,1},{2,6},{6,10},{... | collective-permute-start | bytes 506888 | tf_op jit(solution)/shard_map/ppermute | solution.py:23
  26.3 10.9 %collective-permute-start.3 = (f32[5,22,3,128]{3,2,1,0:T(4,128)S(1)}, f32[5,22,3,128]{3,2,1,0:T(4,128)S(1)}, u32[]{:S(2)}, u32[]{:S(2)}) collective-permute-start(f32[5,22,3,128]{3,2,1,0:T(4,128)S(1)} %get-tuple-element.115), channel_id=1, source_target_pairs={{4,0},{8,4},{12,8},{0,12},{5,1},{9,5},{13,9},{1,13},{6,2},{10,6},{... | collective-permute-start | bytes 506888 | tf_op jit(solution)/shard_map/ppermute | solution.py:24
  36.2 1.4 copy-start.3
  37.2 0.7 copy-start.5
  45.5 16.8 %collective-permute-start.4 = (f32[5,22,38,3]{2,1,3,0:T(8,128)}, f32[5,22,38,3]{2,1,3,0:T(8,128)}, u32[]{:S(2)}, u32[]{:S(2)}) collective-permute-start(f32[5,22,38,3]{2,1,3,0:T(8,128)} %copy.41), channel_id=1, source_target_pairs={{0,1},{1,2},{2,3},{3,0},{4,5},{5,6},{6,7},{7,4},{8,9},{9,10},{10,1... | collective-permute-start | bytes 150488 | tf_op jit(solution)/shard_map/ppermute | solution.py:23
  48.7 16.7 %collective-permute-start.5 = (f32[5,22,38,3]{2,1,3,0:T(8,128)}, f32[5,22,38,3]{2,1,3,0:T(8,128)}, u32[]{:S(2)}, u32[]{:S(2)}) collective-permute-start(f32[5,22,38,3]{2,1,3,0:T(8,128)} %copy.42), channel_id=1, source_target_pairs={{1,0},{2,1},{3,2},{0,3},{5,4},{6,5},{7,6},{4,7},{9,8},{10,9},{11,1... | collective-permute-start | bytes 150488 | tf_op jit(solution)/shard_map/ppermute | solution.py:24
  65.5 3.2 copy-start.4
  65.5 3.2 copy-start.6
  68.7 4.9 %copy-start = (f32[5,22,38,3]{3,2,1,0:T(8,128)S(1)}, f32[5,22,38,3]{3,2,1,0:T(8,128)}, u32[]{:S(2)}) copy-start(f32[5,22,38,3]{3,2,1,0:T(8,128)} %copy.43) | copy-start | bytes 150484
  68.7 4.9 %copy-start.1 = (f32[5,22,38,3]{3,2,1,0:T(8,128)S(1)}, f32[5,22,38,3]{3,2,1,0:T(8,128)}, u32[]{:S(2)}) copy-start(f32[5,22,38,3]{3,2,1,0:T(8,128)} %copy.44) | copy-start | bytes 150484
  79.6 15.4 %copy-start.7 = (f32[5,17,32,128]{3,2,1,0:T(8,128)S(1)}, f32[5,17,32,128]{3,2,1,0:T(8,128)}, u32[]{:S(2)}) copy-start(f32[5,17,32,128]{3,2,1,0:T(8,128)} %divide_add_fusion.2) | copy-start | bytes 4177924
  79.6 15.4 %copy-start.8 = (f32[5,16,33,128]{3,2,1,0:T(8,128)S(1)}, f32[5,16,33,128]{3,2,1,0:T(8,128)}, u32[]{:S(2)}) copy-start(f32[5,16,33,128]{3,2,1,0:T(8,128)} %divide_add_fusion.1) | copy-start | bytes 4055044
  79.6 15.4 %copy-start.11 = (f32[5,16,32,128]{3,2,1,0:T(8,128)S(1)}, f32[5,16,32,128]{3,2,1,0:T(8,128)}, u32[]{:S(2)}) copy-start(f32[5,16,32,128]{3,2,1,0:T(8,128)} %param.11) | copy-start | bytes 3932164
  79.6 15.4 %copy-start.13 = (f32[5,16,32,128]{3,2,1,0:T(8,128)S(1)}, f32[5,16,32,128]{3,2,1,0:T(8,128)}, u32[]{:S(2)}) copy-start(f32[5,16,32,128]{3,2,1,0:T(8,128)} %param.10) | copy-start | bytes 3932164
  95.8 23.1 %copy-start.12 = (f32[5,16,32,128]{3,2,1,0:T(8,128)}, f32[5,16,32,128]{3,2,1,0:T(8,128)S(1)}, u32[]{:S(2)}) copy-start(f32[5,16,32,128]{3,2,1,0:T(8,128)S(1)} %fusion.54) | copy-start | bytes 3932164
  118.9 4.2 %copy-start.9 = (bf16[512,256]{1,0:T(8,128)(2,1)S(1)}, bf16[512,256]{1,0:T(8,128)(2,1)}, u32[]{:S(2)}) copy-start(bf16[512,256]{1,0:T(8,128)(2,1)} %fusion.60) | copy-start | bytes 786436
  163.6 1.0 copy-start.2
  164.6 219.2 %all-reduce.2.cloned.1.call-start = ((), (), s32[]{:S(2)}) async-start(), calls=%async_computation.2 | async-start | bytes 524288 | tf_op jit(solution)/shard_map/psum | solution.py:237
Sparse Core Ops, SparseCore 0:
  164.7 144.6 reduce-scatter.1
  312.8 71.0 all-reduce.1
where the time goes:
time: 394 us; the launch traced here: 392 us
  waiting for transfers between devices  224 us (57%)
  other arithmetic  89 us (23%)
  local copies, waits for them, and re-layouts  45.6 us (12%)
  between operations  15.2 us (4%)
  matrix products  9.54 us (2%)
  starting transfers between devices  8.79 us (2%)
    reduce_scatter x1, waiting for transfers between devices, local(): gz_share = lax.psum_scatter(running, 'gz', scatter_dimension=1, tiled=True)  145 us
    psum x1, waiting for transfers between devices, local(): spectra_out = lax.psum(gz_share, ('gx', 'gy'))  74.4 us
    add x3, other arithmetic, face_difference(): weno_face(split_up[0], split_up[1], split_up[2], split_up[3], split_up[4])  34.9 us
    gather x1, local copies, waits for them, and re-layouts, local(): sampled = density[panel_cell]  23 us
    reduce_sum x2, other arithmetic, observer_group(): jnp.sum(masks * real_part, axis=0)  22 us
    dot_general x2, matrix products, observer_group(): jnp.einsum('gop,gpk->gok', weights, spectra, preferred_element_type=jnp.f...  9.54 us
    concatenate x3, other arithmetic, with_halo(): shard = jnp.concatenate([before, shard, after], axis=dim)  8.06 us
  transfers between devices with their start and end apart: 8, of which 5 were waited for; matrix products, arithmetic and copies ran while one was open for 8% of the time, Pallas kernels for 0%

commit v1 on v0

--- a/solution.py
+++ b/solution.py
@@ -234,7 +234,8 @@
         0, group_total, add_group, jnp.zeros((2, listeners.shape[1], FREQS), jnp.float32)
     )
     gz_share = lax.psum_scatter(running, "gz", scatter_dimension=1, tiled=True)
-    spectra_out = lax.psum(gz_share, ("gx", "gy"))
+    a_next = jax.lax.all_gather(gz_share, axis_name=("gx", "gy"))
+    spectra_out = jnp.sum(a_next, 0)
     return (updated, spectra_out)
 
 

time: 394 us -> 372 us (0.944)
  waiting for transfers between devices: 224 us -> 201 us
    psum x1 -> x0, waiting for transfers between devices: 74.4 us -> none  [local(): spectra_out = lax.psum(gz_share, ('gx', 'gy'))]
    all_gather x0 -> x1, waiting for transfers between devices: none -> 51.2 us  [local(): a_next = jax.lax.all_gather(gz_share, axis_name=('gx', 'gy'))]
  transfers between devices with their start and end apart: 8 -> 8, of which waited for: 5 -> 5; matrix products, arithmetic and copies ran while one was open for 8% -> 9% of each run, Pallas kernels for 0% -> 0%
where the time goes in v1:
time: 372 us; the launch traced here: 370 us
  waiting for transfers between devices  201 us (54%)
  other arithmetic  91.4 us (25%)
  local copies, waits for them, and re-layouts  43.9 us (12%)
  between operations  15.2 us (4%)
  matrix products  9.54 us (3%)
  starting transfers between devices  8.79 us (2%)
    reduce_scatter x1, waiting for transfers between devices, local(): gz_share = lax.psum_scatter(running, 'gz', scatter_dimension=1, tiled=True)  145 us
    all_gather x1, waiting for transfers between devices, local(): a_next = jax.lax.all_gather(gz_share, axis_name=('gx', 'gy'))  51.2 us
    add x3, other arithmetic, face_difference(): weno_face(split_up[0], split_up[1], split_up[2], split_up[3], split_up[4])  34.9 us
    gather x1, local copies, waits for them, and re-layouts, local(): sampled = density[panel_cell]  23 us
    reduce_sum x2, other arithmetic, observer_group(): jnp.sum(masks * real_part, axis=0)  22 us
    dot_general x2, matrix products, observer_group(): jnp.einsum('gop,gpk->gok', weights, spectra, preferred_element_type=jnp.f...  9.54 us
    concatenate x3, other arithmetic, with_halo(): shard = jnp.concatenate([before, shard, after], axis=dim)  8.06 us
  transfers between devices with their start and end apart: 8, of which 5 were waited for; matrix products, arithmetic and copies ran while one was open for 9% of the time, Pallas kernels for 0%

profile of v1, /device:TPU:0, one launch (start us, length us, event | category | flops | bytes accessed | tf_op | source)
XLA Modules:
  0.0 369.9 jit_solution(11389371042494974883)
XLA Ops:
  7.2 1.9 fusion.121
  9.1 3.0 collective-permute-start
  12.8 1.8 multiply_bitcast_fusion.1
  14.6 1.0 cosine_multiply_fusion
  15.6 1.1 fusion.95
  20.3 3.0 collective-permute-done.1
  24.4 1.9 collective-permute-start.2
  26.3 2.1 collective-permute-start.3
  28.4 7.8 %divide_add_fusion.2 = f32[5,17,32,128]{3,2,1,0:T(8,128)} fusion(f32[5,19,32,128]{3,2,1,0:T(8,128)S(1)} %get-tuple-element.123, f32[5,22,32,128]{3,2,1,0:T(8,128)S(1)} %multiply_dynamic-update-slice_fusion.1, f32[5,19,32,128]{3,2,1,0:T(8,128)S(1)} %get-tuple-element.116, f32[17,32,128]{2,1,0:T(8,128)S(1)} %slice_maximum_fusion.10), kind=kLoop, calls=%fused_computation.92 | loop fusion | flops 51179520 | bytes 18382848 | tf_op jit(solution)/shard_map/add | solution.py:102
  36.2 1.0 collective-permute-done.3
  38.0 2.7 fusion.119
  42.2 3.3 copy.41
  45.5 3.3 copy.42
  48.7 1.7 collective-permute-start.5
  50.5 11.8 %divide_add_fusion.1 = f32[5,16,33,128]{3,2,1,0:T(8,128)} fusion(f32[5,22,3,128]{3,2,1,0:T(4,128)} %copy-done.5, f32[5,22,32,128]{3,2,1,0:T(8,128)S(1)} %get-tuple-element.124, f32[5,16,38,128]{3,2,1,0:T(8,128)S(1)} %multiply_dynamic-update-slice_fusion.2, f32[5,22,3,128]{3,2,1,0:T(4,128)} %copy-done.3, f32[16,33,128]{2,1,0:T(8,128)} %slice_maximum_fusion.5), kind=kLoop, calls=%fused_computation.75 | loop fusion | flops 51701760 | bytes 11872256 | tf_op jit(solution)/shard_map/add | solution.py:102
  62.3 3.2 copy.43
  65.5 3.2 copy.44
  68.7 4.9 %pad_maximum_fusion = f32[5,22,38,134]{3,2,1,0:T(8,128)S(1)} fusion(f32[5,22,38,3]{3,2,1,0:T(8,128)} %copy.44, f32[5,22,3,128]{3,2,1,0:T(4,128)S(1)} %copy-done.6, f32[5,22,32,128]{3,2,1,0:T(8,128)S(1)} %get-tuple-element.124, f32[5,22,3,128]{3,2,1,0:T(4,128)S(1)} %copy-done.4, f32[5,22,38,3]{3,2,1,0:T(8,128)} %copy.43), kind=kLoop, calls=%fused_computation.34 | loop fusion | flops 2240480 | bytes 4480960 | tf_op jit(solution)/shard_map/concatenate | solution.py:25
  76.8 2.8 maximum_maximum_fusion
  79.6 15.3 %divide_add_fusion = f32[5,16,32,129]{3,2,1,0:T(8,128)S(1)} fusion(f32[5,22,38,131]{3,2,1,0:T(8,128)S(1)} %get-tuple-element.109, f32[5,16,32,134]{3,2,1,0:T(8,128)S(1)} %multiply_dynamic-update-slice_fusion, f32[5,22,38,131]{3,2,1,0:T(8,128)S(1)} %get-tuple-element.108, f32[16,32,129]{2,1,0:T(8,128)S(1)} %slice_maximum_fusion), kind=kLoop, calls=%fused_computation.49 | loop fusion | flops 48545280 | bytes 17436672 | tf_op jit(solution)/shard_map/add | solution.py:102
  95.8 23.0 %gather_fusion = f32[4096]{0:T(1024)S(1)} fusion(f32[65536]{0:T(1024)S(1)} %bitcast.127, s32[4096]{0:T(1024)S(1)} %fusion.111), kind=kCustom, calls=%fused_computation | custom fusion | bytes 49152 | tf_op jit(solution)/shard_map/gather | solution.py:200
  118.9 4.1 %fusion.23 = bf16[32,128,512]{2,1,0:T(8,128)(2,1)} fusion(bf16[32,128,512]{2,1,0:T(8,128)(2,1)} %bitcast.130, f32[32,128]{1,0:T(8,128)S(1)} %bitcast.135), kind=kLoop, calls=%fused_computation.33 | loop fusion | flops 6291456 | bytes 8404992 | tf_op jit(solution)/shard_map/convert_element_type | solution.py:204
  123.1 40.5 %while.11 = (s32[]{:T(128)}, f32[2,1024,128]{2,1,0:T(8,128)S(1)}, s32[]{:T(128)}, f32[32]{0:T(128)S(1)}, f32[32,6,128]{2,1,0:T(8,128)}, /*index=5*/f32[3,1024]{1...) while((s32[]{:T(128)}, f32[2,1024,128]{2,1,0:T(8,128)S(1)}, ...), condition=%wide.region_10.11_spmd.clone, body=%wide.region_3.10_spmd.clone.sunk | while | flops 417236864 | bytes 21886488 | solution.py:233
  124.2 2.9 fusion.131
  127.1 4.8 %fusion.132 = f32[4,1024,256]{2,1,0:T(8,128)} fusion(f32[4,1024,128]{2,1,0:T(8,128)} %get-tuple-element.195, f32[4,1024,128]{2,1,0:T(8,128)S(1)} %get-tuple-element.196, bf16[32,128,512]{2,1,0:T(8,128)(2,1)} %get-tuple-element.232, s32[]{:T(128)S(6)} %select_n.94, bf16[512,256]{1,0:T(8,128)(2,1)S(1)} %get-tuple-element.233), kind=kOutput, calls=%fused_computation.20.clone.1 | convolution fusion | flops 404357120 | bytes 9175044 | tf_op jit(solution)/shard_map/while/body/gop,gpk->gok/dot_general | solution.py:161
  132.2 11.0 %fusion.133 = (f32[1024,128]{1,0:T(8,128)S(1)}, f32[1024,128]{1,0:T(8,128)S(1)}) fusion(f32[4,1024,256]{2,1,0:T(8,128)} %fusion.132, f32[128]{0:T(128)S(1)} %convert_multiply_fusion.3, f32[4,1024]{1,0:T(4,128)S(1)} %sqrt.30, f32[4]{0:T(128)S(1)} %dynamic_slice.18), kind=kLoop, calls=%fused_computation.14.clone.1 | loop fusion | flops 5505024 | bytes 5259792 | tf_op jit(solution)/shard_map/while/body/reduce_sum | solution.py:172
  144.3 2.9 fusion.131
  147.3 4.8 %fusion.132 = f32[4,1024,256]{2,1,0:T(8,128)} fusion(f32[4,1024,128]{2,1,0:T(8,128)} %get-tuple-element.195, f32[4,1024,128]{2,1,0:T(8,128)S(1)} %get-tuple-element.196, bf16[32,128,512]{2,1,0:T(8,128)(2,1)} %get-tuple-element.232, s32[]{:T(128)S(6)} %select_n.94, bf16[512,256]{1,0:T(8,128)(2,1)S(1)} %get-tuple-element.233), kind=kOutput, calls=%fused_computation.20.clone.1 | convolution fusion | flops 404357120 | bytes 9175044 | tf_op jit(solution)/shard_map/while/body/gop,gpk->gok/dot_general | solution.py:161
  152.4 11.0 %fusion.133 = (f32[1024,128]{1,0:T(8,128)S(1)}, f32[1024,128]{1,0:T(8,128)S(1)}) fusion(f32[4,1024,256]{2,1,0:T(8,128)} %fusion.132, f32[128]{0:T(128)S(1)} %convert_multiply_fusion.3, f32[4,1024]{1,0:T(4,128)S(1)} %sqrt.30, f32[4]{0:T(128)S(1)} %dynamic_slice.18), kind=kLoop, calls=%fused_computation.14.clone.1 | loop fusion | flops 5505024 | bytes 5259792 | tf_op jit(solution)/shard_map/while/body/reduce_sum | solution.py:172
  164.7 144.8 %reduce-scatter.2.cloned.1.call-done = f32[2,256,128]{2,1,0:T(8,128)} async-done(((f32[2,1024,128]{2,1,0:T(8,128)}), f32[2,256,128]{2,1,0:T(8,128)}) %reduce-scatter.2.cloned.1.call-update) | async-done | bytes 262160 | tf_op jit(solution)/shard_map/reduce_scatter | solution.py:236
  309.5 51.2 %all-gather.3.cloned.1.call-done = f32[16,256,128]{2,1,0:T(8,128)} async-done(((f32[2,256,128]{2,1,0:T(8,128)}), f32[16,256,128]{2,1,0:T(8,128)}) %all-gather.3.cloned.1.call-update) | async-done | bytes 2097168 | tf_op jit(solution)/shard_map/all_gather | solution.py:237
  360.7 2.4 reduce_sum.93
  (98 shorter events, 14.7 us)
Async XLA Ops:
  7.2 12.8 %copy-start.10 = (f32[5,16,32,128]{3,2,1,0:T(8,128)S(1)}, f32[5,16,32,128]{3,2,1,0:T(8,128)}, u32[]{:S(2)}) copy-start(f32[5,16,32,128]{3,2,1,0:T(8,128)} %param.11) | copy-start | bytes 3932164
  7.2 10.3 %copy-start.14 = (s32[32,128]{1,0:T(8,128)S(1)}, s32[32,128]{1,0:T(8,128)}, u32[]{:S(2)}) copy-start(s32[32,128]{1,0:T(8,128)} %param.13) | copy-start | bytes 49156
  7.2 11.1 %copy-start.15 = (f32[1024]{0:T(1024)S(1)}, f32[1024]{0:T(1024)}, u32[]{:S(2)}) copy-start(f32[1024]{0:T(1024)} %param.17) | copy-start | bytes 12292
  7.2 302.3 %reduce-scatter.2.cloned.1.call-start = ((), (), s32[]{:S(2)}) async-start(), calls=%async_computation.1 | async-start | bytes 1310720 | tf_op jit(solution)/shard_map/reduce_scatter | solution.py:236
  9.1 9.9 %collective-permute-start = (f32[5,3,32,128]{3,2,1,0:T(8,128)S(1)}, f32[5,3,32,128]{3,2,1,0:T(8,128)}, u32[]{:S(2)}, u32[]{:S(2)}) collective-permute-start(f32[5,3,32,128]{3,2,1,0:T(8,128)S(1)} %get-tuple-element.120), channel_id=1, source_target_pairs={{0,16},{16,0},{1,17},{17,1},{2,18},{18,2},{3,19},{19,3},{4,20},{20... | collective-permute-start | bytes 737288 | tf_op jit(solution)/shard_map/ppermute | solution.py:23
  12.1 11.2 %collective-permute-start.1 = (f32[5,3,32,128]{3,2,1,0:T(8,128)}, f32[5,3,32,128]{3,2,1,0:T(8,128)S(1)}, u32[]{:S(2)}, u32[]{:S(2)}) collective-permute-start(f32[5,3,32,128]{3,2,1,0:T(8,128)} %get-tuple-element.119), channel_id=1, source_target_pairs={{16,0},{0,16},{17,1},{1,17},{18,2},{2,18},{19,3},{3,19},{20,4},{4,... | collective-permute-start | bytes 737288 | tf_op jit(solution)/shard_map/ppermute | solution.py:24
  24.4 11.8 %collective-permute-start.2 = (f32[5,22,3,128]{3,2,1,0:T(4,128)S(1)}, f32[5,22,3,128]{3,2,1,0:T(4,128)S(1)}, u32[]{:S(2)}, u32[]{:S(2)}) collective-permute-start(f32[5,22,3,128]{3,2,1,0:T(4,128)S(1)} %get-tuple-element.114), channel_id=1, source_target_pairs={{0,4},{4,8},{8,12},{12,0},{1,5},{5,9},{9,13},{13,1},{2,6},{6,10},{... | collective-permute-start | bytes 506888 | tf_op jit(solution)/shard_map/ppermute | solution.py:23
  26.3 10.9 %collective-permute-start.3 = (f32[5,22,3,128]{3,2,1,0:T(4,128)S(1)}, f32[5,22,3,128]{3,2,1,0:T(4,128)S(1)}, u32[]{:S(2)}, u32[]{:S(2)}) collective-permute-start(f32[5,22,3,128]{3,2,1,0:T(4,128)S(1)} %get-tuple-element.115), channel_id=1, source_target_pairs={{4,0},{8,4},{12,8},{0,12},{5,1},{9,5},{13,9},{1,13},{6,2},{10,6},{... | collective-permute-start | bytes 506888 | tf_op jit(solution)/shard_map/ppermute | solution.py:24
  36.2 1.4 copy-start.3
  37.2 0.7 copy-start.5
  45.5 16.8 %collective-permute-start.4 = (f32[5,22,38,3]{2,1,3,0:T(8,128)}, f32[5,22,38,3]{2,1,3,0:T(8,128)}, u32[]{:S(2)}, u32[]{:S(2)}) collective-permute-start(f32[5,22,38,3]{2,1,3,0:T(8,128)} %copy.41), channel_id=1, source_target_pairs={{0,1},{1,2},{2,3},{3,0},{4,5},{5,6},{6,7},{7,4},{8,9},{9,10},{10,1... | collective-permute-start | bytes 150488 | tf_op jit(solution)/shard_map/ppermute | solution.py:23
  48.7 16.7 %collective-permute-start.5 = (f32[5,22,38,3]{2,1,3,0:T(8,128)}, f32[5,22,38,3]{2,1,3,0:T(8,128)}, u32[]{:S(2)}, u32[]{:S(2)}) collective-permute-start(f32[5,22,38,3]{2,1,3,0:T(8,128)} %copy.42), channel_id=1, source_target_pairs={{1,0},{2,1},{3,2},{0,3},{5,4},{6,5},{7,6},{4,7},{9,8},{10,9},{11,1... | collective-permute-start | bytes 150488 | tf_op jit(solution)/shard_map/ppermute | solution.py:24
  65.5 3.2 copy-start.4
  65.5 3.2 copy-start.6
  68.7 4.9 %copy-start = (f32[5,22,38,3]{3,2,1,0:T(8,128)S(1)}, f32[5,22,38,3]{3,2,1,0:T(8,128)}, u32[]{:S(2)}) copy-start(f32[5,22,38,3]{3,2,1,0:T(8,128)} %copy.43) | copy-start | bytes 150484
  68.7 4.9 %copy-start.1 = (f32[5,22,38,3]{3,2,1,0:T(8,128)S(1)}, f32[5,22,38,3]{3,2,1,0:T(8,128)}, u32[]{:S(2)}) copy-start(f32[5,22,38,3]{3,2,1,0:T(8,128)} %copy.44) | copy-start | bytes 150484
  79.6 15.4 %copy-start.7 = (f32[5,17,32,128]{3,2,1,0:T(8,128)S(1)}, f32[5,17,32,128]{3,2,1,0:T(8,128)}, u32[]{:S(2)}) copy-start(f32[5,17,32,128]{3,2,1,0:T(8,128)} %divide_add_fusion.2) | copy-start | bytes 4177924
  79.6 15.4 %copy-start.8 = (f32[5,16,33,128]{3,2,1,0:T(8,128)S(1)}, f32[5,16,33,128]{3,2,1,0:T(8,128)}, u32[]{:S(2)}) copy-start(f32[5,16,33,128]{3,2,1,0:T(8,128)} %divide_add_fusion.1) | copy-start | bytes 4055044
  79.6 15.4 %copy-start.11 = (f32[5,16,32,128]{3,2,1,0:T(8,128)S(1)}, f32[5,16,32,128]{3,2,1,0:T(8,128)}, u32[]{:S(2)}) copy-start(f32[5,16,32,128]{3,2,1,0:T(8,128)} %param.11) | copy-start | bytes 3932164
  79.6 15.4 %copy-start.13 = (f32[5,16,32,128]{3,2,1,0:T(8,128)S(1)}, f32[5,16,32,128]{3,2,1,0:T(8,128)}, u32[]{:S(2)}) copy-start(f32[5,16,32,128]{3,2,1,0:T(8,128)} %param.10) | copy-start | bytes 3932164
  95.8 23.1 %copy-start.12 = (f32[5,16,32,128]{3,2,1,0:T(8,128)}, f32[5,16,32,128]{3,2,1,0:T(8,128)S(1)}, u32[]{:S(2)}) copy-start(f32[5,16,32,128]{3,2,1,0:T(8,128)S(1)} %fusion.54) | copy-start | bytes 3932164
  118.9 4.2 %copy-start.9 = (bf16[512,256]{1,0:T(8,128)(2,1)S(1)}, bf16[512,256]{1,0:T(8,128)(2,1)}, u32[]{:S(2)}) copy-start(bf16[512,256]{1,0:T(8,128)(2,1)} %fusion.60) | copy-start | bytes 786436
  163.6 1.0 copy-start.2
  164.6 196.1 %all-gather.3.cloned.1.call-start = ((), (), s32[]{:S(2)}) async-start(), calls=%async_computation.2 | async-start | bytes 2359296 | tf_op jit(solution)/shard_map/all_gather | solution.py:237
Sparse Core Ops, SparseCore 0:
  164.7 144.6 reduce-scatter.1
  311.6 49.0 all-gather.2
